TPU v7x, 32 devices: a whole 2x2x4 slice. The times are simulated.
32 devices in a mesh: prow: 4 (over z), pcol: 8 (over y, x, core).
Axes of the slice: x: 2, y: 2, z: 4, core: 2. Of those that a mesh axis runs over, the one named last changes fastest.
Arguments:
- values: float32 [12, 4, 4, 8, 256, 256], P(None, 'prow', None, 'pcol'), may hold values from -6 to 6
- pattern: int32 [12, 4, 4, 8], P(None, 'prow', None, 'pcol'), may hold values from 0 to 1
Outputs:
- factored: float32 [12, 4, 4, 8, 256, 256], P(None, 'prow', None, 'pcol')
All inputs are finite; a program needn't handle non-finite values.
Results may differ from a plain program's by a relative error of at most 0.0003.
Values sent between devices are 32-bit elements; how exact they have to be, the bound alone decides.
No kernel may reach another device: no remote copies, remote signals or barrier semaphores. Data moves between devices by JAX's collectives and lax.ppermute only.
A program may use at most 128 MiB of HBM per device.

v0:
```python
import math
import jax
import jax.numpy as jnp
from jax import lax
from jax.sharding import PartitionSpec as P

SWEEPS = 3
shift_coef = 5.0


def spread(value, axis, source):
    kept = jnp.where(lax.axis_index(axis) == source, value, 0).astype(value.dtype)
    return lax.psum(kept, axis)


def newton(block, shift):
    width = block.shape[0]
    eye = jnp.eye(width, dtype=jnp.float32)
    approx = eye / shift
    for step in range(SWEEPS):
        inner = jnp.dot(block, approx, precision=lax.Precision.HIGHEST)
        approx = jnp.dot(approx, 2.0 * eye - inner, precision=lax.Precision.HIGHEST)
    return approx


def spread_inverse(block, shift, root_row):
    return spread(newton(block, shift), "prow", root_row)


def apply_panel(blocks, rows_g, cols_g, mult, upper, k):
    product = jnp.einsum("rab,cbe->rcae", mult, upper, precision=lax.Precision.HIGHEST)
    below = rows_g > k
    trail = (below[:, None] & (cols_g > k)[None, :])[:, :, None, None]
    store = (below[:, None] & (cols_g == k)[None, :])[:, :, None, None]
    out = jnp.where(trail, blocks - product, blocks)
    return jnp.where(store, mult[:, None], out)


def drop_one(array, index, axis_pos):
    return jnp.concatenate(
        [
            lax.slice_in_dim(array, 0, index, axis=axis_pos),
            lax.slice_in_dim(array, index + 1, array.shape[axis_pos], axis=axis_pos),
        ],
        axis=axis_pos,
    )


def put_one(array, piece, index, axis_pos):
    return jnp.concatenate(
        [lax.slice_in_dim(array, 0, index, axis=axis_pos), piece, array], axis=axis_pos
    )


def factor_panel(column, row, k, shift, nprow, npcol):
    root_row, loc_row = (k % nprow, k // nprow)
    root_col = k % npcol
    inverse = spread_inverse(column[loc_row], shift, root_row)
    mult = jnp.einsum("rab,be->rae", column, inverse, precision=lax.Precision.HIGHEST)
    mult = spread(mult, "pcol", root_col)
    upper = spread(row, "prow", root_row)
    return (mult, upper)


def body(values, pattern):
    rows_loc, cols_loc, width = (values.shape[0], values.shape[2], values.shape[4])
    nprow = lax.axis_size("prow")
    npcol = lax.axis_size("pcol")
    rows_g = jnp.arange(rows_loc, dtype=jnp.int32) * nprow + lax.axis_index("prow")
    cols_g = jnp.arange(cols_loc, dtype=jnp.int32) * npcol + lax.axis_index("pcol")
    shift = shift_coef * math.sqrt(width)
    eye = jnp.eye(width, dtype=jnp.float32)
    blocks = values[:, 0, :, 0] * pattern[:, 0, :, 0].astype(jnp.float32)[:, :, None, None]
    diag = jnp.where(rows_g[:, None] == cols_g[None, :], shift, 0.0).astype(jnp.float32)
    blocks = blocks + diag[:, :, None, None] * eye
    row_first, col_first = (0 // nprow, 0 // npcol)
    row_next, col_next = (1 // nprow, 1 // npcol)
    mult_first, upper_first = factor_panel(
        blocks[:, col_first], blocks[row_first], 0, shift, nprow, npcol
    )
    column = apply_panel(
        blocks[:, col_next : col_next + 1],
        rows_g,
        cols_g[col_next : col_next + 1],
        mult_first,
        upper_first[col_next : col_next + 1],
        0,
    )[:, 0]
    row = apply_panel(
        blocks[row_next : row_next + 1],
        rows_g[row_next : row_next + 1],
        cols_g,
        mult_first[row_next : row_next + 1],
        upper_first,
        0,
    )[0]
    mult_next, upper_next = factor_panel(column, row, 1, shift, nprow, npcol)
    inner = drop_one(drop_one(blocks, row_next, 0), col_next, 1)
    inner = apply_panel(
        inner,
        drop_one(rows_g, row_next, 0),
        drop_one(cols_g, col_next, 0),
        drop_one(mult_first, row_next, 0),
        drop_one(upper_first, col_next, 0),
        0,
    )
    inner = put_one(inner, drop_one(column, row_next, 0)[:, None], col_next, 1)
    blocks = put_one(inner, row[None], row_next, 0)
    blocks = apply_panel(blocks, rows_g, cols_g, mult_next, upper_next, 1)
    return blocks[:, None, :, None]


def solution(mesh):
    placed = (P(None, "prow", None, "pcol", None, None), P(None, "prow", None, "pcol"))
    return jax.shard_map(
        body,
        mesh=mesh,
        in_specs=placed,
        out_specs=P(None, "prow", None, "pcol", None, None),
        check_vma=False,
    )
```

profile of v0, /device:TPU:0, one launch (start us, length us, event | category | flops | bytes accessed | tf_op | source)
XLA Modules:
  0.0 351.3 jit_solution(18210090547723713760)
XLA Ops:
  6.5 0.0 all-reduce.13.cloned.1.call-start
  6.6 0.7 convert_element_type.28
  7.3 0.1 compare_select_fusion
  7.4 12.2 %fusion.2 = f32[12,4,256,256]{3,2,0,1:T(8,128)} fusion(f32[12,1,4,1,256,256]{5,4,3,2,1,0:T(8,128)} %param.2, f32[256,256]{1,0:T(8,128)S(1)} %fusion.29, f32[12,4]{0,1:T(4,128)S(1)} %compare_select_fusion, f32[12,4]{0,1:T(4,128)S(1)} %bitcast.102), kind=kLoop, calls=%fused_computation.5 | loop fusion | flops 9437184 | bytes 25428352 | tf_op jit(solution)/shard_map/add | solution.py:75
  19.6 1.3 convolution_subtract_fusion.5
  20.9 0.4 fusion.23
  21.3 1.3 convolution_subtract_fusion.4
  22.6 0.4 fusion.47
  23.0 1.3 convolution_subtract_fusion.3
  24.4 2.3 select_bitcast_fusion.1
  26.7 1.1 convolution_select_fusion.1
  27.8 0.0 all-reduce.13.cloned.1.call-update
  27.8 0.0 all-reduce.7.cloned.1.call-start
  27.8 62.9 %all-reduce.13.cloned.1.call-done = (f32[256,256]{1,0:T(8,128)}, f32[4,256,256]{2,1,0:T(8,128)}) async-done(((f32[256,256]{1,0:T(8,128)}, f32[4,256,256]{2,1,0:T(8,128)}), (f32[256,256]{1,0:T(8,128)}, f32[4,256,256]{2,1,0:T(8,128)})) %all-reduce.13.cloned.1.call-update) | async-done | bytes 1310736 | tf_op jit(solution)/shard_map/psum | solution.py:13
  90.8 6.2 %fusion.12 = f32[12,256,256]{2,1,0:T(8,128)} fusion(f32[12,4,256,256]{3,2,0,1:T(8,128)} %fusion.2, pred[]{:T(512)S(6)} %eq.84, f32[256,256]{1,0:T(8,128)} %get-tuple-element.7), kind=kOutput, calls=%fused_computation.16 | convolution fusion | flops 2416705536 | bytes 6553601 | tf_op jit(solution)/shard_map/rab,be->rae/dot_general | solution.py:59
  97.0 0.0 all-reduce.7.cloned.1.call-update
  97.0 0.2 all-reduce.11.cloned.1.call-start
  97.4 68.7 %all-reduce.7.cloned.1.call-done = f32[12,256,256]{2,1,0:T(8,128)} async-done(((f32[12,256,256]{2,1,0:T(8,128)}), f32[12,256,256]{2,1,0:T(8,128)}) %all-reduce.7.cloned.1.call-update) | async-done | bytes 3145744 | tf_op jit(solution)/shard_map/psum | solution.py:13
  166.1 6.6 %fusion.4 = f32[12,1,256,256]{3,2,0,1:T(8,128)S(1)} fusion(f32[12,256,256]{2,1,0:T(8,128)} %all-reduce.7.cloned.1.call-done, f32[12,4,256,256]{3,2,0,1:T(8,128)} %fusion.2, pred[12]{0:T(512)(128)(4,1)S(1)} %get-tuple-element.15, pred[12]{0:T(512)(128)(4,1)S(1)} %get-tuple-element.16, f32[4,256,256]{2,1,0:T(8,128)} %get-tuple-element.8), kind=kOutput, calls=%fused_computation.8 | convolution fusion | flops 2418278400 | bytes 12845080 | tf_op jit(solution)/shard_map/rab,cbe->rcae/dot_general | solution.py:31
  172.7 0.0 copy-start
  172.7 0.0 copy-start.1
  172.7 0.4 convolution_subtract_fusion.2
  173.1 0.4 fusion.20
  173.5 0.4 convolution_subtract_fusion.1
  173.9 0.4 fusion.48
  174.2 0.4 convolution_subtract_fusion
  174.6 1.1 copy-done.1
  175.7 0.0 copy-done.2
  175.7 2.4 fusion.18
  178.1 1.1 copy-done.4
  179.2 1.1 select_bitcast_fusion
  180.3 1.1 convolution_select_fusion
  181.3 0.0 all-reduce.11.cloned.1.call-update
  181.4 0.0 all-reduce.9.cloned.1.call-start
  181.4 0.1 slice_compare_fusion
  181.5 60.2 %all-reduce.11.cloned.1.call-done = (f32[256,256]{1,0:T(8,128)}, f32[4,256,256]{2,1,0:T(8,128)}) async-done(((f32[256,256]{1,0:T(8,128)}, f32[4,256,256]{2,1,0:T(8,128)}), (f32[256,256]{1,0:T(8,128)}, f32[4,256,256]{2,1,0:T(8,128)})) %all-reduce.11.cloned.1.call-update) | async-done | bytes 1310736 | tf_op jit(solution)/shard_map/psum | solution.py:13
  241.7 5.3 %fusion.15 = f32[12,256,256]{2,1,0:T(8,128)} fusion(f32[12,1,256,256]{3,2,0,1:T(8,128)S(1)} %fusion.4, pred[]{:T(512)S(6)} %eq.82, f32[256,256]{1,0:T(8,128)} %get-tuple-element.5), kind=kOutput, calls=%fused_computation.17 | convolution fusion | flops 2416705536 | bytes 6553601 | tf_op jit(solution)/shard_map/rab,be->rae/dot_general | solution.py:59
  246.9 0.0 all-reduce.9.cloned.1.call-update
  247.0 0.1 slice_compare_fusion.2
  247.1 0.1 broadcast_and_fusion.3
  247.1 0.1 broadcast_and_fusion.1
  247.2 1.8 slice-done.1
  249.0 0.3 copy-done.3
  249.3 11.9 %fusion.3 = f32[11,3,256,256]{3,2,0,1:T(8,128)} fusion(f32[12,4,256,256]{3,2,0,1:T(8,128)} %fusion.2, f32[11,256,256]{2,1,0:T(8,128)S(1)} %slice-done.1, pred[11,3]{0,1:T(4,128)(4,1)S(1)} %get-tuple-element.12, pred[11,3]{0,1:T(4,128)(4,1)S(1)} %get-tuple-element.11, f32[4,256,256]{2,1,0:T(8,128)S(1)} %copy-done.3), kind=kOutput, calls=%fused_computation.6 | convolution fusion | flops 6650265600 | bytes 23856128 | tf_op jit(solution)/shard_map/rab,cbe->rcae/dot_general | solution.py:31
  261.2 54.8 %all-reduce.9.cloned.1.call-done = f32[12,256,256]{2,1,0:T(8,128)} async-done(((f32[12,256,256]{2,1,0:T(8,128)}), f32[12,256,256]{2,1,0:T(8,128)}) %all-reduce.9.cloned.1.call-update) | async-done | bytes 3145744 | tf_op jit(solution)/shard_map/psum | solution.py:13
  316.0 0.0 slice-done
  316.0 18.0 %fusion.1 = f32[12,1,4,1,256,256]{5,4,0,2,3,1:T(8,128)} fusion(f32[11,3,256,256]{3,2,0,1:T(8,128)} %fusion.3, f32[11,1,256,256]{3,2,0,1:T(8,128)S(1)} %slice-done, f32[1,4,256,256]{3,2,0,1:T(8,128)} %copy-done.4, f32[12,256,256]{2,1,0:T(8,128)} %all-reduce.9.cloned.1.call-done, pred[12,4]{0,1:T(4,128)(4,1)S(1)} %get-tuple-element.10, ...), kind=kOutput, calls=%fused_computation.3 | convolution fusion | flops 9679405056 | bytes 29360224 | tf_op jit(solution)/shard_map/rab,cbe->rcae/dot_general | solution.py:31
  334.0 10.8 %copy.12 = f32[12,1,4,1,256,256]{5,4,3,2,1,0:T(8,128)} copy(f32[12,1,4,1,256,256]{5,4,0,2,3,1:T(8,128)} %fusion.1) | data formatting | bytes 25165824 | tf_op jit(solution)/shard_map/broadcast_in_dim | solution.py:110
  (14 shorter events, 0.1 us)
Async XLA Ops:
  6.5 84.2 %all-reduce.13.cloned.1.call-start = ((), (), s32[]{:S(2)}) async-start(), calls=%async_computation.3 | async-start | bytes 2621440 | tf_op jit(solution)/shard_map/psum | solution.py:13
  27.8 138.3 %all-reduce.7.cloned.1.call-start = ((), (), s32[]{:S(2)}) async-start(), calls=%async_computation | async-start | bytes 6291456 | tf_op jit(solution)/shard_map/psum | solution.py:13
  97.0 144.7 %all-reduce.11.cloned.1.call-start = ((), (), s32[]{:S(2)}) async-start(), calls=%async_computation.2 | async-start | bytes 2621440 | tf_op jit(solution)/shard_map/psum | solution.py:13
  166.0 9.7 %copy-start.2 = (f32[4,256,256]{2,1,0:T(8,128)S(1)}, f32[4,256,256]{2,1,0:T(8,128)}, u32[]{:S(2)}) copy-start(f32[4,256,256]{2,1,0:T(8,128)} %get-tuple-element.8) | copy-start | bytes 3145732
  172.7 74.5 %copy-start = (f32[12,1,256,256]{3,2,0,1:T(8,128)}, f32[12,1,256,256]{3,2,0,1:T(8,128)S(1)}, u32[]{:S(2)}) copy-start(f32[12,1,256,256]{3,2,0,1:T(8,128)S(1)} %fusion.4) | copy-start | bytes 9437188
  172.7 3.0 copy-start.1
  178.1 1.1 copy-start.4
  181.4 134.6 %all-reduce.9.cloned.1.call-start = ((), (), s32[]{:S(2)}) async-start(), calls=%async_computation.1 | async-start | bytes 6291456 | tf_op jit(solution)/shard_map/psum | solution.py:13
  247.2 1.8 slice-start.1
  247.2 2.1 copy-start.3
  249.3 66.7 %slice-start = ((f32[12,1,256,256]{3,2,0,1:T(8,128)}), f32[11,1,256,256]{3,2,0,1:T(8,128)S(1)}, s32[]{:S(2)}) async-start(f32[12,1,256,256]{3,2,0,1:T(8,128)} %copy-done), calls=%async_computation.4 | async-start | bytes 5767168 | tf_op jit(solution)/shard_map/slice | solution.py:43
Sparse Core Ops, SparseCore 0:
  27.9 62.8 all-reduce.12
  97.1 68.8 all-reduce.6
  181.5 60.1 all-reduce.10
  247.1 68.8 all-reduce.8
where the time goes:
time: 352 us; the launch traced here: 351 us
  waiting for transfers between devices  247 us (70%)
  matrix products  59.1 us (17%)
  other arithmetic  16.7 us (5%)
  local copies, waits for them, and re-layouts  15 us (4%)
  between operations  13.4 us (4%)
    psum x4, waiting for transfers between devices, spread(): return lax.psum(kept, axis)  247 us
    dot_general x4, matrix products, apply_panel(): jnp.einsum('rab,cbe->rcae', mult, upper, precision=lax.Precision.HIGHEST)  38.8 us
    add x1, other arithmetic, body(): blocks = blocks + diag[:, :, None, None] * eye  12.2 us
    dot_general x2, matrix products, factor_panel(): jnp.einsum('rab,be->rae', column, inverse, precision=lax.Precision.HIGHEST)  11.5 us
    broadcast_in_dim x1, local copies, waits for them, and re-layouts, body(): return blocks[:, None, :, None]  10.8 us
  transfers between devices with their start and end apart: 4, of which 4 were waited for; matrix products, arithmetic and copies ran while one was open for 3% of the time, Pallas kernels for 0%

commit v1 on v0

--- a/solution.py
+++ b/solution.py
@@ -10,7 +10,7 @@
 
 def spread(value, axis, source):
     kept = jnp.where(lax.axis_index(axis) == source, value, 0).astype(value.dtype)
-    return lax.psum(kept, axis)
+    return jnp.sum(lax.all_gather(kept, axis), axis=0)
 
 
 def newton(block, shift):

time: 352 us -> 567 us (1.61)
  waiting for transfers between devices: 247 us -> 430 us
  other arithmetic: 16.7 us -> 47.9 us
    all_gather x0 -> x6, waiting for transfers between devices: none -> 430 us  [spread(): return jnp.sum(lax.all_gather(kept, axis), axis=0)]
    psum x4 -> x0, waiting for transfers between devices: 247 us -> none  [spread(): return lax.psum(kept, axis)]
    reduce_sum x0 -> x6, other arithmetic: none -> 32.3 us  [spread(): return jnp.sum(lax.all_gather(kept, axis), axis=0)]
  transfers between devices with their start and end apart: 4 -> 6, of which waited for: 4 -> 6; matrix products, arithmetic and copies ran while one was open for 3% -> 7% of each run, Pallas kernels for 0% -> 0%
where the time goes in v1:
time: 567 us
  waiting for transfers between devices  430 us (76%)
  matrix products  59.9 us (11%)
  other arithmetic  47.9 us (8%)
  local copies, waits for them, and re-layouts  14.1 us (2%)
  between operations  13.8 us (2%)
    all_gather x6, waiting for transfers between devices, spread(): return jnp.sum(lax.all_gather(kept, axis), axis=0)  430 us
    dot_general x4, matrix products, apply_panel(): jnp.einsum('rab,cbe->rcae', mult, upper, precision=lax.Precision.HIGHEST)  40.6 us
    reduce_sum x6, other arithmetic, spread(): return jnp.sum(lax.all_gather(kept, axis), axis=0)  32.3 us
    add x1, other arithmetic, body(): blocks = blocks + diag[:, :, None, None] * eye  12.2 us
  transfers between devices with their start and end apart: 6, of which 6 were waited for; matrix products, arithmetic and copies ran while one was open for 7% of the time, Pallas kernels for 0%

profile of v1, /device:TPU:0, one launch (start us, length us, event | category | flops | bytes accessed | tf_op | source)
XLA Modules:
  0.0 566.6 jit_solution(5117417723005870117)
XLA Ops:
  6.6 0.7 convert_element_type.28
  7.3 0.1 compare_select_fusion
  7.3 12.2 %fusion.2 = f32[12,4,256,256]{3,2,0,1:T(8,128)} fusion(f32[12,1,4,1,256,256]{5,4,3,2,1,0:T(8,128)} %param.2, f32[256,256]{1,0:T(8,128)S(1)} %fusion.29, f32[12,4]{0,1:T(4,128)S(1)} %compare_select_fusion, f32[12,4]{0,1:T(4,128)S(1)} %bitcast.109), kind=kLoop, calls=%fused_computation.5 | loop fusion | flops 9437184 | bytes 25428352 | tf_op jit(solution)/shard_map/add | solution.py:75
  19.6 1.3 convolution_subtract_fusion.5
  20.9 0.4 fusion.23
  21.3 1.3 convolution_subtract_fusion.4
  22.6 0.4 fusion.47
  23.0 1.3 convolution_subtract_fusion.3
  24.4 1.1 convolution_select_fusion.1
  25.5 0.0 all-gather.15.cloned.1.call-update
  25.5 0.0 all-gather.11.cloned.1.call-start
  25.5 2.3 slice_select_fusion
  27.9 0.0 all-gather.17.cloned.1.call-start
  27.9 28.4 %all-gather.15.cloned.1.call-done = f32[1024,256]{1,0:T(8,128)} async-done(((f32[256,256]{1,0:T(8,128)}), f32[1024,256]{1,0:T(8,128)}) %all-gather.15.cloned.1.call-update) | async-done | bytes 1048592 | tf_op jit(solution)/shard_map/all_gather | solution.py:13
  56.3 1.3 reduce_sum.54
  57.7 6.2 %fusion.12 = f32[12,256,256]{2,1,0:T(8,128)} fusion(f32[12,4,256,256]{3,2,0,1:T(8,128)} %fusion.2, pred[]{:T(512)S(6)} %eq.84, f32[256,256]{1,0:T(8,128)S(1)} %reduce_sum.54), kind=kOutput, calls=%fused_computation.16 | convolution fusion | flops 2416705536 | bytes 6553601 | tf_op jit(solution)/shard_map/rab,be->rae/dot_general | solution.py:59
  63.8 0.2 all-gather.19.cloned.1.call-start
  64.2 73.9 %all-gather.11.cloned.1.call-done = f32[4,4,256,256]{3,2,0,1:T(8,128)} async-done(((f32[1,4,256,256]{3,2,0,1:T(8,128)}), f32[4,4,256,256]{3,2,0,1:T(8,128)}) %all-gather.11.cloned.1.call-update) | async-done | bytes 4194320 | tf_op jit(solution)/shard_map/all_gather | solution.py:13
  138.1 3.6 reduce_sum.56
  141.6 122.0 %all-gather.17.cloned.1.call-done = f32[96,256,256]{2,1,0:T(8,128)} async-done(((f32[12,256,256]{2,1,0:T(8,128)}), f32[96,256,256]{2,1,0:T(8,128)}) %all-gather.17.cloned.1.call-update) | async-done | bytes 25165840 | tf_op jit(solution)/shard_map/all_gather | solution.py:13
  263.7 11.2 %reduce_sum.55 = f32[12,256,256]{2,1,0:T(8,128)} reduce(f32[8,12,256,256]{3,2,1,0:T(8,128)} %bitcast.106, f32[]{:T(128)} %constant.8.clone.1), dimensions={0}, to_apply=%region_1.2 | reduce | flops 5505024 | bytes 28311556 | tf_op jit(solution)/shard_map/reduce_sum | solution.py:13
  274.9 6.6 %fusion.4 = f32[12,1,256,256]{3,2,0,1:T(8,128)S(1)} fusion(f32[12,256,256]{2,1,0:T(8,128)} %reduce_sum.55, f32[12,4,256,256]{3,2,0,1:T(8,128)} %fusion.2, pred[12]{0:T(512)(128)(4,1)S(1)} %get-tuple-element.13, pred[12]{0:T(512)(128)(4,1)S(1)} %get-tuple-element.14, f32[4,256,256]{2,1,0:T(8,128)} %reduce_sum.56), kind=kOutput, calls=%fused_computation.8 | convolution fusion | flops 2418278400 | bytes 12845080 | tf_op jit(solution)/shard_map/rab,cbe->rcae/dot_general | solution.py:31
  281.5 0.4 convolution_subtract_fusion.2
  281.9 0.4 fusion.20
  282.3 0.4 convolution_subtract_fusion.1
  282.6 0.4 fusion.48
  283.0 0.4 convolution_subtract_fusion
  283.4 1.1 convolution_select_fusion
  284.5 0.0 all-gather.13.cloned.1.call-start
  284.6 1.0 slice_bitcast_fusion.6
  285.6 4.2 broadcast_select_fusion
  289.8 0.0 all-gather.21.cloned.1.call-start
  289.8 22.8 %all-gather.19.cloned.1.call-done = f32[1024,256]{1,0:T(8,128)} async-done(((f32[256,256]{1,0:T(8,128)}), f32[1024,256]{1,0:T(8,128)}) %all-gather.19.cloned.1.call-update) | async-done | bytes 1048592 | tf_op jit(solution)/shard_map/all_gather | solution.py:13
  312.7 1.3 reduce_sum.57
  314.0 4.3 fusion.15
  318.3 0.1 slice_compare_fusion
  318.4 0.1 slice_compare_fusion.2
  318.5 0.1 broadcast_and_fusion.1
  318.6 0.1 broadcast_and_fusion.3
  318.7 2.0 slice-done.1
  320.7 0.4 copy-done.1
  321.1 11.9 %fusion.3 = f32[11,3,256,256]{3,2,0,1:T(8,128)} fusion(f32[12,4,256,256]{3,2,0,1:T(8,128)} %fusion.2, f32[11,256,256]{2,1,0:T(8,128)S(1)} %slice-done.1, pred[11,3]{0,1:T(4,128)(4,1)S(1)} %get-tuple-element.8, pred[11,3]{0,1:T(4,128)(4,1)S(1)} %get-tuple-element.7, f32[4,256,256]{2,1,0:T(8,128)S(1)} %copy-done.1), kind=kOutput, calls=%fused_computation.6 | convolution fusion | flops 6650265600 | bytes 23856128 | tf_op jit(solution)/shard_map/rab,cbe->rcae/dot_general | solution.py:31
  332.9 61.3 %all-gather.13.cloned.1.call-done = f32[4,4,256,256]{3,2,0,1:T(8,128)} async-done(((f32[1,4,256,256]{3,2,0,1:T(8,128)}), f32[4,4,256,256]{3,2,0,1:T(8,128)}) %all-gather.13.cloned.1.call-update) | async-done | bytes 4194320 | tf_op jit(solution)/shard_map/all_gather | solution.py:13
  394.2 3.6 reduce_sum.59
  397.8 121.9 %all-gather.21.cloned.1.call-done = f32[96,256,256]{2,1,0:T(8,128)} async-done(((f32[12,256,256]{2,1,0:T(8,128)}), f32[96,256,256]{2,1,0:T(8,128)}) %all-gather.21.cloned.1.call-update) | async-done | bytes 25165840 | tf_op jit(solution)/shard_map/all_gather | solution.py:13
  519.7 11.3 %reduce_sum.58 = f32[12,256,256]{2,1,0:T(8,128)} reduce(f32[8,12,256,256]{3,2,1,0:T(8,128)} %bitcast.105, f32[]{:T(128)} %constant.8.clone.1), dimensions={0}, to_apply=%region_4.5 | reduce | flops 5505024 | bytes 28311556 | tf_op jit(solution)/shard_map/reduce_sum | solution.py:13
  531.0 18.0 %fusion.1 = f32[12,1,4,1,256,256]{5,4,0,2,3,1:T(8,128)} fusion(f32[11,3,256,256]{3,2,0,1:T(8,128)} %fusion.3, f32[11,1,256,256]{3,2,0,1:T(8,128)S(1)} %slice-done, f32[1,4,256,256]{3,2,0,1:T(8,128)} %get-tuple-element.12, f32[12,256,256]{2,1,0:T(8,128)} %reduce_sum.58, pred[12,4]{0,1:T(4,128)(4,1)S(1)} %get-tuple-element.6, ...), kind=kOutput, calls=%fused_computation.3 | convolution fusion | flops 9679405056 | bytes 29360224 | tf_op jit(solution)/shard_map/rab,cbe->rcae/dot_general | solution.py:31
  549.0 10.8 %copy.18 = f32[12,1,4,1,256,256]{5,4,3,2,1,0:T(8,128)} copy(f32[12,1,4,1,256,256]{5,4,0,2,3,1:T(8,128)} %fusion.1) | data formatting | bytes 25165824 | tf_op jit(solution)/shard_map/broadcast_in_dim | solution.py:110
  (19 shorter events, 0.2 us)
Async XLA Ops:
  6.5 49.8 %all-gather.15.cloned.1.call-start = ((), (), s32[]{:S(2)}) async-start(), calls=%async_computation.2 | async-start | bytes 1310720 | tf_op jit(solution)/shard_map/all_gather | solution.py:13
  25.5 112.6 %all-gather.11.cloned.1.call-start = ((), (), s32[]{:S(2)}) async-start(), calls=%async_computation | async-start | bytes 5242880 | tf_op jit(solution)/shard_map/all_gather | solution.py:13
  27.9 235.8 %all-gather.17.cloned.1.call-start = ((), (), s32[]{:S(2)}) async-start(), calls=%async_computation.3 | async-start | bytes 28311552 | tf_op jit(solution)/shard_map/all_gather | solution.py:13
  63.8 248.8 %all-gather.19.cloned.1.call-start = ((), (), s32[]{:S(2)}) async-start(), calls=%async_computation.4 | async-start | bytes 1310720 | tf_op jit(solution)/shard_map/all_gather | solution.py:13
  281.5 37.2 %copy-start = (f32[12,1,256,256]{3,2,0,1:T(8,128)}, f32[12,1,256,256]{3,2,0,1:T(8,128)S(1)}, u32[]{:S(2)}) copy-start(f32[12,1,256,256]{3,2,0,1:T(8,128)S(1)} %fusion.4) | copy-start | bytes 9437188
  284.5 109.7 %all-gather.13.cloned.1.call-start = ((), (), s32[]{:S(2)}) async-start(), calls=%async_computation.1 | async-start | bytes 5242880 | tf_op jit(solution)/shard_map/all_gather | solution.py:13
  289.8 229.9 %all-gather.21.cloned.1.call-start = ((), (), s32[]{:S(2)}) async-start(), calls=%async_computation.5 | async-start | bytes 28311552 | tf_op jit(solution)/shard_map/all_gather | solution.py:13
  318.7 2.0 slice-start.1
  318.7 2.4 copy-start.1
  519.7 11.3 %slice-start = ((f32[12,1,256,256]{3,2,0,1:T(8,128)}), f32[11,1,256,256]{3,2,0,1:T(8,128)S(1)}, s32[]{:S(2)}) async-start(f32[12,1,256,256]{3,2,0,1:T(8,128)} %copy-done), calls=%async_computation.6 | async-start | bytes 5767168 | tf_op jit(solution)/shard_map/slice | solution.py:43
Sparse Core Ops, SparseCore 0:
  25.6 30.6 all-gather.14
  57.9 80.1 all-gather.10
  140.0 123.6 all-gather.16
  284.7 27.9 all-gather.18
  314.1 80.1 all-gather.12
  396.0 123.6 all-gather.20
